TPU v7x, 32 devices: a whole 2x2x4 slice. The times are simulated.
32 devices in a mesh: row: 8 (over y, x, core), col: 4 (over z).
Axes of the slice: x: 2, y: 2, z: 4, core: 2. Of those that a mesh axis runs over, the one named last changes fastest.
Arguments:
- singular_vectors: float32 [4096, 4096], P('row', 'col'), may hold values from -6 to 6
- reflector_vectors: float32 [2, 16, 256, 512], P(None, 'row', 'col'), may hold values from -2 to 2, as said below
- reflector_factors: float32 [2, 16, 256, 256], P(None, 'row', 'col'), as said below
- sweep_bounds: int32 [2, 2], replicated, may hold values from 0 to 3584, as said below
Outputs:
- transformed: float32 [4096, 4096], P('row', 'col')
Inputs may be any that keep to these rules, and one draw needn't show every extreme that they name: `reflector_vectors`: row j of each block's 256 x 2 * 256 slice is a reflector: 1 at position j, nonzero only at positions j to j + 255. `reflector_factors`: each block's factor is the upper triangular inverse of the strictly upper part of W W^T plus half of its diagonal, W being that block's slice of reflector_vectors, so that each block's transformation is orthogonal. `sweep_bounds`: both entries are multiples of 256, and the first is below the second.
All inputs are finite; a program needn't handle non-finite values.
Results may differ from a plain program's by a relative error of at most 0.0003.
Values sent between devices are 32-bit elements; how exact they have to be, the bound alone decides.
A program may use at most 64 MiB of HBM per device.

v0:
```python
import functools

import jax
import jax.numpy as jnp
from jax import lax
from jax.experimental import pallas as pl
from jax.experimental.pallas import tpu as pltpu
from jax.sharding import PartitionSpec as P

MESH = pl.DeviceIdType.MESH
f32, bf16 = jnp.float32, jnp.bfloat16
WIDTH = 128


def split(value):
    high = value.astype(bf16)
    return high, (value - high.astype(f32)).astype(bf16)


def dot3(a, b):
    (a_high, a_low), (b_high, b_low) = a, b
    dot = functools.partial(jnp.dot, preferred_element_type=f32)
    return dot(a_high, b_high) + (dot(a_high, b_low) + dot(a_low, b_high))


def kernel(
    count, ring, bounds_ref, x_ref, vec_ref, fac_ref, out_ref,
    gathered, upper_high, upper_low, lower_high, lower_low,
    below, tops, returned, back, middle,
    hop_send, hop_recv, far_send, far_recv, up_send, up_recv, down_send, down_recv,
):
    me, slab = lax.axis_index("row"), lax.axis_index("col")
    bw = gathered.shape[2]
    part = bw // ring
    pieces, width = below.shape[1], below.shape[3]
    first, last = me == 0, me == count - 1

    def block_rows(owner):
        return pl.ds(pl.multiple_of(owner * part, part), part)

    for s in range(2):
        for b in range(2):
            w = vec_ref[s, b]
            gathered[s, b, block_rows(slab), :bw] = w[:, :bw] + w[:, bw:]
            gathered[s, b, block_rows(slab), bw:] = fac_ref[s, b]

    @pl.when(last)
    def _():
        below[...] = jnp.zeros_like(below)

    barrier = pltpu.get_barrier_semaphore()

    @pl.when(jnp.logical_not(first))
    def _():
        pl.semaphore_signal(barrier, inc=1, device_id={"row": me - 1}, device_id_type=MESH)

    @pl.when(jnp.logical_not(last))
    def _():
        pl.semaphore_signal(barrier, inc=1, device_id={"row": me + 1}, device_id_type=MESH)

    for k in range(1, ring):
        pl.semaphore_signal(
            barrier, inc=1, device_id={"col": lax.rem(slab + k, ring)}, device_id_type=MESH
        )
    peers = jnp.where(me > 0, 1, 0) + jnp.where(me < count - 1, 1, 0) + ring - 1
    pl.semaphore_wait(barrier, peers)

    def hop(way, t, owner):
        block = gathered.at[0, :, block_rows(owner)]
        return pltpu.make_async_remote_copy(
            src_ref=block, dst_ref=block,
            send_sem=hop_send.at[way, t], recv_sem=hop_recv.at[way, t],
            device_id={"col": slab + (1 - 2 * way)}, device_id_type=MESH,
        )

    def sends(way, t):
        if way == 0:
            return (slab - t >= 0) & (slab + 1 < ring)
        return (slab + t < ring) & (slab >= 1)

    def gets(way, t):
        return slab - 1 - t >= 0 if way == 0 else slab + 1 + t < ring

    for t in range(ring - 1):
        for way in range(2):
            sign = 1 - 2 * way

            @pl.when(sends(way, t))
            def _():
                hop(way, t, slab - sign * t).start()

        for way in range(2):
            sign = 1 - 2 * way

            @pl.when(gets(way, t))
            def _():
                hop(way, t, slab - sign * (t + 1)).wait_recv()

    def far(k, owner):
        block = gathered.at[1, :, block_rows(owner)]
        return pltpu.make_async_remote_copy(
            src_ref=block, dst_ref=block,
            send_sem=far_send.at[k], recv_sem=far_recv.at[k],
            device_id={"col": lax.rem(slab + k, ring)}, device_id_type=MESH,
        )

    for k in range(1, ring):
        far(k, slab).start()

    def build(s):
        row = lax.broadcasted_iota(jnp.int32, (bw, bw), 0)
        col = lax.broadcasted_iota(jnp.int32, (bw, bw), 1)
        row2 = lax.broadcasted_iota(jnp.int32, (2 * bw, 2 * bw), 0)
        col2 = lax.broadcasted_iota(jnp.int32, (2 * bw, 2 * bw), 1)
        unit = jnp.where(row2 == col2, 1.0, 0.0).astype(f32)

        def whole(b):
            start = (me * 2 + b) * bw
            live = (start >= bounds_ref[s, 0]) & (start <= bounds_ref[s, 1])
            packed = gathered[s, b, :, :bw]
            factor = gathered[s, b, :, bw:] * jnp.where(live, 1.0, 0.0).astype(f32)
            w_t = jnp.concatenate(
                [jnp.where(col >= row, packed, 0.0), jnp.where(col < row, packed, 0.0)], axis=1
            )
            g = dot3(split(factor), split(w_t))
            return unit - dot3(split(w_t.T), split(g))

        q1 = whole(1)
        lower_high[s], lower_low[s] = split(q1[bw:])
        q0 = whole(0)
        mixed = dot3(split(q0[:, bw:]), split(q1[:bw]))
        upper_high[s, :, :bw], upper_low[s, :, :bw] = split(q0[:, :bw])
        upper_high[s, :, bw:], upper_low[s, :, bw:] = split(mixed)

    def columns(p):
        return pl.ds(pl.multiple_of(p * width, width), width)

    def up(s, p):
        return pltpu.make_async_remote_copy(
            src_ref=tops.at[s, p], dst_ref=below.at[s, p],
            send_sem=up_send.at[s, p], recv_sem=up_recv.at[s, p],
            device_id={"row": me - 1}, device_id_type=MESH,
        )

    def down(s, p):
        target = back.at[p] if s == 0 else out_ref.at[pl.ds(0, bw), columns(p)]
        return pltpu.make_async_remote_copy(
            src_ref=returned.at[s, p], dst_ref=target,
            send_sem=down_send.at[s, p], recv_sem=down_recv.at[s, p],
            device_id={"row": me + 1}, device_id_type=MESH,
        )

    def sweep(s):
        def piece(p, carry):
            if s == 0:
                x0, x1 = x_ref[:bw, columns(p)], x_ref[bw:, columns(p)]
            else:
                @pl.when(jnp.logical_not(first))
                def _():
                    down(0, p).wait_recv()

                x0, x1 = back[p], middle[p]

            @pl.when(jnp.logical_not(last))
            def _():
                up(s, p).wait_recv()

            parts = split(jnp.concatenate([x0, x1, below[s, p]], axis=0))
            tops[s, p] = dot3((upper_high[s, :bw], upper_low[s, :bw]), parts)

            @pl.when(jnp.logical_not(first))
            def _():
                up(s, p).start()

            tail = tuple(value[bw:] for value in parts)
            returned[s, p] = dot3((lower_high[s], lower_low[s]), tail)

            @pl.when(jnp.logical_not(last))
            def _():
                down(s, p).start()

            kept = dot3((upper_high[s, bw:], upper_low[s, bw:]), parts)
            if s == 0:
                middle[p] = kept

                @pl.when(first)
                def _():
                    back[p] = tops[s, p]
            else:
                out_ref[bw:, columns(p)] = kept

                @pl.when(first)
                def _():
                    out_ref[:bw, columns(p)] = tops[s, p]

            return carry

        lax.fori_loop(0, pieces, piece, 0)

    build(0)
    sweep(0)
    for k in range(1, ring):
        far(k, lax.rem(slab + ring - k, ring)).wait_recv()
    build(1)
    sweep(1)

    for t in range(ring - 1):
        for way in range(2):
            @pl.when(sends(way, t))
            def _():
                hop(way, t, slab).wait_send()

    for k in range(1, ring):
        far(k, slab).wait_send()

    def finish(p, carry):
        @pl.when(jnp.logical_not(first))
        def _():
            up(0, p).wait_send()
            up(1, p).wait_send()
            down(1, p).wait_recv()

        @pl.when(jnp.logical_not(last))
        def _():
            down(0, p).wait_send()
            down(1, p).wait_send()

        return carry

    lax.fori_loop(0, pieces, finish, 0)


def per_device(singular_vectors, reflector_vectors, reflector_factors, sweep_bounds):
    count, ring = lax.axis_size("row"), lax.axis_size("col")
    rows, cols = singular_vectors.shape
    sweeps, blocks, _, span = reflector_vectors.shape
    bw = span // 2
    assert sweeps == 2 and blocks == 2 and rows == span and cols % WIDTH == 0
    pieces = cols // WIDTH
    vmem, dma = pltpu.VMEM, pltpu.SemaphoreType.DMA
    return pl.pallas_call(
        functools.partial(kernel, count, ring),
        out_shape=jax.ShapeDtypeStruct((rows, cols), f32),
        in_specs=[pl.BlockSpec(memory_space=pltpu.SMEM)] + [pl.BlockSpec(memory_space=vmem)] * 3,
        out_specs=pl.BlockSpec(memory_space=vmem),
        scratch_shapes=[
            vmem((2, 2, bw, span), f32),
            vmem((2, span, 3 * bw), bf16), vmem((2, span, 3 * bw), bf16),
            vmem((2, bw, span), bf16), vmem((2, bw, span), bf16),
            vmem((2, pieces, bw, WIDTH), f32),
            vmem((2, pieces, bw, WIDTH), f32),
            vmem((2, pieces, bw, WIDTH), f32),
            vmem((pieces, bw, WIDTH), f32),
            vmem((pieces, bw, WIDTH), f32),
            dma((2, ring)), dma((2, ring)), dma((ring,)), dma((ring,)),
            dma((2, pieces)), dma((2, pieces)), dma((2, pieces)), dma((2, pieces)),
        ],
        compiler_params=pltpu.CompilerParams(
            collective_id=0, has_side_effects=True, vmem_limit_bytes=56 * 2**20
        ),
    )(sweep_bounds, singular_vectors, reflector_vectors, reflector_factors)


def solution(mesh):
    placed = (P("row", "col"), P(None, "row", "col", None), P(None, "row", "col", None), P())
    return jax.shard_map(
        per_device, mesh=mesh, in_specs=placed, out_specs=P("row", "col"), check_vma=False
    )
```

profile of v0, /device:TPU:0, one launch (start us, length us, event | category | flops | bytes accessed | tf_op | source)
XLA Modules:
  0.0 107.7 jit_solution(6515184779224235619)
XLA Ops:
  0.0 104.5 %shard_map.46 = f32[512,1024]{1,0:T(8,128)} custom-call(s32[2,2]{1,0:T(2,128)} %bounds_ref.1, f32[512,1024]{1,0:T(8,128)} %x_ref.1, f32[2,2,64,512]{3,2,1,0:T(8,128)} %vec_ref.1, f32[2,2,64,256]{3,2,1,0:T(8,128)} %fac_ref.1), custom_call_target="tpu_custom_call" | custom-call | tf_op jit(solution)/shard_map/pallas_call | solution.py:241
  104.5 3.2 %copy.6 = f32[512,1024]{1,0:T(8,128)} copy(f32[512,1024]{1,0:T(8,128)} %shard_map.46) | data formatting | bytes 4194304
where the time goes:
time: 108 us
  Pallas kernels  105 us (97%)
  local copies, waits for them, and re-layouts  3.16 us (3%)
    pallas_call x1, Pallas kernels, per_device(): pl.pallas_call(functools.partial(kernel, count, ring), out_shape=jax.Shap...  105 us
    unnamed x1, local copies, waits for them, and re-layouts  3.16 us

commit v1 on v0

v1 whole, which is shorter than its diff:
```python
import functools

import jax
import jax.numpy as jnp
from jax import lax
from jax.experimental import pallas as pl
from jax.experimental.pallas import tpu as pltpu
from jax.sharding import PartitionSpec as P

MESH = pl.DeviceIdType.MESH
f32, bf16 = jnp.float32, jnp.bfloat16
WIDTH = 128


def split(value):
    high = value.astype(bf16)
    return high, (value - high.astype(f32)).astype(bf16)


def dot3(a, b):
    (a_high, a_low), (b_high, b_low) = a, b
    dot = functools.partial(jnp.dot, preferred_element_type=f32)
    return dot(a_high, b_high) + (dot(a_high, b_low) + dot(a_low, b_high))


def kernel(
    count, ring, bounds_ref, x_ref, vec_ref, fac_ref, out_ref,
    gathered, outbox, upper_high, upper_low, lower_high, lower_low,
    prev, below, tops, returned, middle,
    shift_send, shift_recv, hop_send, hop_recv, far_send, far_recv,
    first_send, first_recv, up_send, up_recv, down_send, down_recv,
):
    me, slab = lax.axis_index("row"), lax.axis_index("col")
    bw = x_ref.shape[0] // 2
    half = bw // 2
    part = bw // ring
    pieces, width = below.shape[1], below.shape[3]
    first, last = me == 0, me == count - 1

    def block_rows(owner):
        return pl.ds(pl.multiple_of(owner * part, part), part)

    def columns(p):
        return pl.ds(pl.multiple_of(p * width, width), width)

    barrier = pltpu.get_barrier_semaphore()

    @pl.when(jnp.logical_not(first))
    def _():
        pl.semaphore_signal(barrier, inc=1, device_id={"row": me - 1}, device_id_type=MESH)

    @pl.when(jnp.logical_not(last))
    def _():
        pl.semaphore_signal(barrier, inc=1, device_id={"row": me + 1}, device_id_type=MESH)

    for k in range(1, ring):
        pl.semaphore_signal(
            barrier, inc=1, device_id={"col": lax.rem(slab + k, ring)}, device_id_type=MESH
        )

    for s in range(2):
        for b, rows in ((1, outbox.at[s]), (0, gathered.at[s, 0, block_rows(slab)])):
            w, f = vec_ref[s, b], fac_ref[s, b]
            rows[:, :bw] = w[:, :bw] + w[:, bw:]
            rows[:, bw:] = jnp.where(slab * part < half, f[:, :half], f[:, half:])

    @pl.when(first)
    def _():
        for s in range(2):
            gathered[s, 1, block_rows(slab)] = jnp.zeros((part, bw + half), f32)
        prev[...] = jnp.zeros_like(prev)

    @pl.when(last)
    def _():
        for p in range(pieces):
            below[0, p] = x_ref[bw:, p * width:(p + 1) * width]

    peers = jnp.where(me > 0, 1, 0) + jnp.where(me < count - 1, 1, 0) + ring - 1
    pl.semaphore_wait(barrier, peers)

    def shift(s):
        return pltpu.make_async_remote_copy(
            src_ref=outbox.at[s], dst_ref=gathered.at[s, 1, block_rows(slab)],
            send_sem=shift_send.at[s], recv_sem=shift_recv.at[s],
            device_id={"row": me + 1}, device_id_type=MESH,
        )

    def initial(p):
        return pltpu.make_async_remote_copy(
            src_ref=x_ref.at[pl.ds(bw, bw), columns(p)], dst_ref=prev.at[0, p],
            send_sem=first_send.at[p], recv_sem=first_recv.at[p],
            device_id={"row": me + 1}, device_id_type=MESH,
        )

    def hop(way, role, t, owner):
        block = gathered.at[0, role, block_rows(owner)]
        return pltpu.make_async_remote_copy(
            src_ref=block, dst_ref=block,
            send_sem=hop_send.at[way, role, t], recv_sem=hop_recv.at[way, role, t],
            device_id={"col": slab + (1 - 2 * way)}, device_id_type=MESH,
        )

    def sends(way, t):
        if way == 0:
            return (slab - t >= 0) & (slab + 1 < ring)
        return (slab + t < ring) & (slab >= 1)

    def gets(way, t):
        return slab - 1 - t >= 0 if way == 0 else slab + 1 + t < ring

    def send_hops(role, t):
        for way in range(2):
            @pl.when(sends(way, t))
            def _():
                hop(way, role, t, slab - (1 - 2 * way) * t).start()

    def get_hops(role, t):
        for way in range(2):
            @pl.when(gets(way, t))
            def _():
                hop(way, role, t, slab - (1 - 2 * way) * (t + 1)).wait_recv()

    def far(role, k, owner):
        block = gathered.at[1, role, block_rows(owner)]
        return pltpu.make_async_remote_copy(
            src_ref=block, dst_ref=block,
            send_sem=far_send.at[role, k], recv_sem=far_recv.at[role, k],
            device_id={"col": lax.rem(slab + k, ring)}, device_id_type=MESH,
        )

    send_hops(0, 0)

    @pl.when(jnp.logical_not(last))
    def _():
        shift(0).start()
        shift(1).start()
        for p in range(pieces):
            initial(p).start()

    @pl.when(jnp.logical_not(first))
    def _():
        shift(0).wait_recv()

    send_hops(1, 0)
    for t in range(ring - 1):
        for role in range(2):
            get_hops(role, t)
            if t + 1 < ring - 1:
                send_hops(role, t + 1)

    @pl.when(jnp.logical_not(first))
    def _():
        shift(1).wait_recv()

    for role in range(2):
        for k in range(1, ring):
            far(role, k, slab).start()

    def build(s):
        row = lax.broadcasted_iota(jnp.int32, (bw, bw), 0)
        col = lax.broadcasted_iota(jnp.int32, (bw, bw), 1)
        row2 = lax.broadcasted_iota(jnp.int32, (2 * bw, 2 * bw), 0)
        col2 = lax.broadcasted_iota(jnp.int32, (2 * bw, 2 * bw), 1)
        unit = jnp.where(row2 == col2, 1.0, 0.0).astype(f32)

        def whole(role):
            start = (me * 2 - role) * bw
            live = (start >= bounds_ref[s, 0]) & (start <= bounds_ref[s, 1])
            packed = gathered[s, role, :, :bw]
            factor = gathered[s, role, :, bw:] * jnp.where(live, 1.0, 0.0).astype(f32)
            w = jnp.concatenate(
                [jnp.where(col >= row, packed, 0.0), jnp.where(col < row, packed, 0.0)], axis=1
            )
            w_high, w_low = split(w)
            head, tail = (w_high[:half], w_low[:half]), (w_high[half:], w_low[half:])
            g_tail = dot3(split(factor[half:]), tail)
            u = dot3(head, tuple(value.T for value in tail))
            g_head = dot3(split(factor[:half]), split(w[:half] - dot3(split(u), split(g_tail))))
            g = jnp.concatenate([g_head, g_tail], axis=0)
            return unit - dot3((w_high.T, w_low.T), split(g))

        q1 = whole(0)
        lower_high[s], lower_low[s] = split(q1[bw:])
        q0 = whole(1)
        mixed = dot3(split(q0[:, bw:]), split(q1[:bw]))
        upper_high[s, :, :bw], upper_low[s, :, :bw] = split(q0[:, :bw])
        upper_high[s, :, bw:], upper_low[s, :, bw:] = split(mixed)

    def up(s, p):
        return pltpu.make_async_remote_copy(
            src_ref=tops.at[s, p], dst_ref=below.at[s, p],
            send_sem=up_send.at[s, p], recv_sem=up_recv.at[s, p],
            device_id={"row": me - 1}, device_id_type=MESH,
        )

    def down(p):
        return pltpu.make_async_remote_copy(
            src_ref=returned.at[p], dst_ref=prev.at[1, p],
            send_sem=down_send.at[p], recv_sem=down_recv.at[p],
            device_id={"row": me + 1}, device_id_type=MESH,
        )

    def sweep(s):
        def piece(p, carry):
            @pl.when(jnp.logical_not(first))
            def _():
                (initial(p) if s == 0 else down(p)).wait_recv()

            @pl.when(jnp.logical_not(last))
            def _():
                up(s, p).wait_recv()

            x0 = x_ref[:bw, columns(p)] if s == 0 else middle[p]
            parts = split(jnp.concatenate([prev[s, p], x0, below[s, p]], axis=0))
            tops[s, p] = dot3((upper_high[s, :bw], upper_low[s, :bw]), parts)

            @pl.when(jnp.logical_not(first))
            def _():
                up(s, p).start()

            ended = dot3((lower_high[s], lower_low[s]), tuple(value[bw:] for value in parts))
            if s == 0:
                returned[p] = ended

                @pl.when(jnp.logical_not(last))
                def _():
                    down(p).start()

                @pl.when(last)
                def _():
                    below[1, p] = returned[p]
            else:
                out_ref[bw:, columns(p)] = ended

            kept = dot3((upper_high[s, bw:], upper_low[s, bw:]), parts)
            if s == 0:
                middle[p] = kept
            else:
                out_ref[:bw, columns(p)] = kept

            return carry

        lax.fori_loop(0, pieces, piece, 0)

    build(0)
    sweep(0)
    for role in range(2):
        for k in range(1, ring):
            far(role, k, lax.rem(slab + ring - k, ring)).wait_recv()
    build(1)
    sweep(1)

    for role in range(2):
        for t in range(ring - 1):
            for way in range(2):
                @pl.when(sends(way, t))
                def _():
                    hop(way, role, t, slab).wait_send()

        for k in range(1, ring):
            far(role, k, slab).wait_send()

    @pl.when(jnp.logical_not(last))
    def _():
        shift(0).wait_send()
        shift(1).wait_send()

    def finish(p, carry):
        @pl.when(jnp.logical_not(first))
        def _():
            up(0, p).wait_send()
            up(1, p).wait_send()

        @pl.when(jnp.logical_not(last))
        def _():
            initial(p).wait_send()
            down(p).wait_send()

        return carry

    lax.fori_loop(0, pieces, finish, 0)


def per_device(singular_vectors, reflector_vectors, reflector_factors, sweep_bounds):
    count, ring = lax.axis_size("row"), lax.axis_size("col")
    rows, cols = singular_vectors.shape
    sweeps, blocks, _, span = reflector_vectors.shape
    bw = span // 2
    assert sweeps == 2 and blocks == 2 and rows == span and cols % WIDTH == 0
    pieces = cols // WIDTH
    vmem, dma = pltpu.VMEM, pltpu.SemaphoreType.DMA
    return pl.pallas_call(
        functools.partial(kernel, count, ring),
        out_shape=jax.ShapeDtypeStruct((rows, cols), f32),
        in_specs=[pl.BlockSpec(memory_space=pltpu.SMEM)] + [pl.BlockSpec(memory_space=vmem)] * 3,
        out_specs=pl.BlockSpec(memory_space=vmem),
        scratch_shapes=[
            vmem((2, 2, bw, bw + bw // 2), f32),
            vmem((2, bw // ring, bw + bw // 2), f32),
            vmem((2, span, 3 * bw), bf16), vmem((2, span, 3 * bw), bf16),
            vmem((2, bw, span), bf16), vmem((2, bw, span), bf16),
            vmem((2, pieces, bw, WIDTH), f32),
            vmem((2, pieces, bw, WIDTH), f32),
            vmem((2, pieces, bw, WIDTH), f32),
            vmem((pieces, bw, WIDTH), f32),
            vmem((pieces, bw, WIDTH), f32),
            dma((2,)), dma((2,)), dma((2, 2, ring)), dma((2, 2, ring)),
            dma((2, ring)), dma((2, ring)), dma((pieces,)), dma((pieces,)),
            dma((2, pieces)), dma((2, pieces)), dma((pieces,)), dma((pieces,)),
        ],
        compiler_params=pltpu.CompilerParams(
            collective_id=0, has_side_effects=True, vmem_limit_bytes=56 * 2**20
        ),
    )(sweep_bounds, singular_vectors, reflector_vectors, reflector_factors)


def solution(mesh):
    placed = (P("row", "col"), P(None, "row", "col", None), P(None, "row", "col", None), P())
    return jax.shard_map(
        per_device, mesh=mesh, in_specs=placed, out_specs=P("row", "col"), check_vma=False
    )
```

time: 108 us -> 89 us (0.82)
  Pallas kernels: 105 us -> 85.7 us
    pallas_call x1, Pallas kernels: 105 us -> 85.7 us  [per_device(): pl.pallas_call(functools.partial(kernel, count, ring), out_shape=jax.Shap...]
where the time goes in v1:
time: 89 us; the launch traced here: 88.9 us
  Pallas kernels  85.7 us (96%)
  local copies, waits for them, and re-layouts  3.16 us (4%)
    pallas_call x1, Pallas kernels, per_device(): pl.pallas_call(functools.partial(kernel, count, ring), out_shape=jax.Shap...  85.7 us
    unnamed x1, local copies, waits for them, and re-layouts  3.16 us

profile of v1, /device:TPU:0, one launch (start us, length us, event | category | flops | bytes accessed | tf_op | source)
XLA Modules:
  0.0 88.9 jit_solution(18350252693846497814)
XLA Ops:
  0.0 85.7 %shard_map.46 = f32[512,1024]{1,0:T(8,128)} custom-call(s32[2,2]{1,0:T(2,128)} %bounds_ref.1, f32[512,1024]{1,0:T(8,128)} %x_ref.1, f32[2,2,64,512]{3,2,1,0:T(8,128)} %vec_ref.1, f32[2,2,64,256]{3,2,1,0:T(8,128)} %fac_ref.1), custom_call_target="tpu_custom_call" | custom-call | tf_op jit(solution)/shard_map/pallas_call | solution.py:292
  85.7 3.2 %copy.6 = f32[512,1024]{1,0:T(8,128)} copy(f32[512,1024]{1,0:T(8,128)} %shard_map.46) | data formatting | bytes 4194304

commit v2 on v0

v2 whole, which is shorter than its diff:
```python
import functools

import jax
import jax.numpy as jnp
from jax import lax
from jax.experimental import pallas as pl
from jax.experimental.pallas import tpu as pltpu
from jax.sharding import PartitionSpec as P

MESH = pl.DeviceIdType.MESH
f32, bf16 = jnp.float32, jnp.bfloat16
WIDTH = 128


def split(value):
    high = value.astype(bf16)
    return high, (value - high.astype(f32)).astype(bf16)


def dot3(a, b):
    (a_high, a_low), (b_high, b_low) = a, b
    dot = functools.partial(jnp.dot, preferred_element_type=f32)
    return dot(a_high, b_high) + (dot(a_high, b_low) + dot(a_low, b_high))


LOW0, UP0, LOW1, UP1, EXTRA = range(5)
LAG = 2


def kernel(
    count, ring, bounds_ref, x_ref, vec_ref, fac_ref, out_ref,
    gathered, outbox, upper_high, upper_low, lower_high, lower_low, extra_high, extra_low,
    window, below, tops,
    shift_send, shift_recv, hop_send, hop_recv,
    first_send, first_recv, up_send, up_recv,
):
    me, slab = lax.axis_index("row"), lax.axis_index("col")
    bw = x_ref.shape[0] // 2
    half = bw // 2
    part = bw // ring
    pieces, width = below.shape[1], below.shape[3]
    first, last = me == 0, me == count - 1
    inner = jnp.logical_not(first)

    def block_rows(owner):
        return pl.ds(pl.multiple_of(owner * part, part), part)

    def columns(p):
        return pl.ds(pl.multiple_of(p * width, width), width)

    barrier = pltpu.get_barrier_semaphore()

    @pl.when(inner)
    def _():
        pl.semaphore_signal(barrier, inc=1, device_id={"row": me - 1}, device_id_type=MESH)

    @pl.when(jnp.logical_not(last))
    def _():
        pl.semaphore_signal(barrier, inc=1, device_id={"row": me + 1}, device_id_type=MESH)

    for way in range(2):
        @pl.when(slab + 1 < ring if way == 0 else slab >= 1)
        def _():
            pl.semaphore_signal(
                barrier, inc=1, device_id={"col": slab + (1 - 2 * way)}, device_id_type=MESH
            )

    def stage(rows, s, b):
        w, f = vec_ref[s, b], fac_ref[s, b]
        rows[:, :bw] = w[:, :bw] + w[:, bw:]
        rows[:, bw:] = jnp.where(slab * part < half, f[:, :half], f[:, half:])

    moved = ((LOW0, 0, 1), (UP0, 0, 0), (UP1, 1, 1))
    for k, (slot, s, b) in enumerate(moved):
        stage(outbox.at[k], s, b)
    stage(gathered.at[LOW1, block_rows(slab)], 1, 0)

    @pl.when(last)
    def _():
        stage(gathered.at[EXTRA, block_rows(slab)], 0, 0)

    @pl.when(first)
    def _():
        gathered[UP1] = jnp.zeros((bw, bw + half), f32)
        window[0] = jnp.zeros_like(window[0])

    def greeted(there):
        return jnp.where(there, 1, 0)

    pl.semaphore_wait(
        barrier,
        greeted(me > 0) + greeted(me < count - 1) + greeted(slab > 0) + greeted(slab < ring - 1),
    )

    def shift(k):
        return pltpu.make_async_remote_copy(
            src_ref=outbox.at[k], dst_ref=gathered.at[moved[k][0], block_rows(slab)],
            send_sem=shift_send.at[k], recv_sem=shift_recv.at[k],
            device_id={"row": me + 1}, device_id_type=MESH,
        )

    def initial(h, p):
        return pltpu.make_async_remote_copy(
            src_ref=x_ref.at[pl.ds(h * bw, bw), columns(p)], dst_ref=window.at[h, p],
            send_sem=first_send.at[h, p], recv_sem=first_recv.at[h, p],
            device_id={"row": me + 1}, device_id_type=MESH,
        )

    def hop(way, slot, t, owner):
        block = gathered.at[slot, block_rows(owner)]
        return pltpu.make_async_remote_copy(
            src_ref=block, dst_ref=block,
            send_sem=hop_send.at[way, slot, t], recv_sem=hop_recv.at[way, slot, t],
            device_id={"col": slab + (1 - 2 * way)}, device_id_type=MESH,
        )

    def sends(way, t):
        if way == 0:
            return (slab - t >= 0) & (slab + 1 < ring)
        return (slab + t < ring) & (slab >= 1)

    def gets(way, t):
        return slab - 1 - t >= 0 if way == 0 else slab + 1 + t < ring

    def send_hops(slot, t, when):
        for way in range(2):
            @pl.when(when & (t < ring - 1) & sends(way, t))
            def _():
                hop(way, slot, t, slab - (1 - 2 * way) * t).start()

    def get_hops(slot, t, when):
        for way in range(2):
            @pl.when(when & gets(way, t))
            def _():
                hop(way, slot, t, slab - (1 - 2 * way) * (t + 1)).wait_recv()

    send_hops(EXTRA, 0, last)

    @pl.when(jnp.logical_not(last))
    def _():
        for k in range(len(moved)):
            shift(k).start()
        for p in range(pieces):
            for h in range(2):
                initial(h, p).start()

    for k, slot in enumerate((LOW0, UP0)):
        @pl.when(inner)
        def _():
            shift(k).wait_recv()

        send_hops(slot, 0, inner)

    for t in range(ring - 1):
        for slot in (EXTRA, LOW0, UP0):
            if t == ring - 2 and slot == UP0:
                break
            when = last if slot == EXTRA else inner
            get_hops(slot, t, when)
            send_hops(slot, t + 1, when)

    send_hops(LOW1, 0, slab >= 0)

    @pl.when(inner)
    def _():
        shift(2).wait_recv()

    send_hops(UP1, 0, inner)

    def whole(slot, s, block):
        row = lax.broadcasted_iota(jnp.int32, (bw, bw), 0)
        col = lax.broadcasted_iota(jnp.int32, (bw, bw), 1)
        row2 = lax.broadcasted_iota(jnp.int32, (2 * bw, 2 * bw), 0)
        col2 = lax.broadcasted_iota(jnp.int32, (2 * bw, 2 * bw), 1)
        unit = jnp.where(row2 == col2, 1.0, 0.0).astype(f32)
        start = block * bw
        live = (start >= bounds_ref[s, 0]) & (start <= bounds_ref[s, 1])
        packed = gathered[slot, :, :bw]
        factor = gathered[slot, :, bw:] * jnp.where(live, 1.0, 0.0).astype(f32)
        w = jnp.concatenate(
            [jnp.where(col >= row, packed, 0.0), jnp.where(col < row, packed, 0.0)], axis=1
        )
        w_high, w_low = split(w)
        head, tail = (w_high[:half], w_low[:half]), (w_high[half:], w_low[half:])
        g_tail = dot3(split(factor[half:]), tail)
        u = dot3(head, tuple(value.T for value in tail))
        g_head = dot3(split(factor[:half]), split(w[:half] - dot3(split(u), split(g_tail))))
        g = jnp.concatenate([g_head, g_tail], axis=0)
        return unit - dot3((w_high.T, w_low.T), split(g))

    def build_low(s):
        lower_high[s], lower_low[s] = split(whole(2 * s, s, 2 * me - 1 + s))

    def build_up(s):
        q = whole(2 * s + 1, s, 2 * me - 2 + s)
        mixed = dot3(split(q[:, bw:]), (lower_high[s, :bw], lower_low[s, :bw]))
        upper_high[s, :, :bw], upper_low[s, :, :bw] = split(q[:, :bw])
        upper_high[s, :, bw:], upper_low[s, :, bw:] = split(mixed)

    @pl.when(last)
    def _():
        extra_high[...], extra_low[...] = split(whole(EXTRA, 0, 2 * me))

        def own(p, carry):
            both = dot3((extra_high[...], extra_low[...]), split(x_ref[:, columns(p)]))
            below[0, p], below[1, p] = both[:bw], both[bw:]
            return carry

        lax.fori_loop(0, pieces, own, 0)

    @pl.when(inner)
    def _():
        build_low(0)

    get_hops(UP0, ring - 2, inner)

    @pl.when(inner)
    def _():
        build_up(0)

    def up(s, p):
        return pltpu.make_async_remote_copy(
            src_ref=tops.at[s, p], dst_ref=below.at[s, p],
            send_sem=up_send.at[s, p], recv_sem=up_recv.at[s, p],
            device_id={"row": me - 1}, device_id_type=MESH,
        )

    def second(q, carry):
        t, slot = q // 2, LOW1 + q % 2
        when = inner | (slot == LOW1)
        get_hops(slot, t, when)
        send_hops(slot, t + 1, when)
        return carry

    def apply(s, p):
        parts = split(jnp.concatenate([window[0, p], window[1, p], below[s, p]], axis=0))

        @pl.when(inner)
        def _():
            tops[s, p] = dot3((upper_high[s, :bw], upper_low[s, :bw]), parts)
            up(s, p).start()

        ended = dot3((lower_high[s, bw:], lower_low[s, bw:]), tuple(value[bw:] for value in parts))
        kept = dot3((upper_high[s, bw:], upper_low[s, bw:]), parts)
        if s == 0:
            window[0, p], window[1, p] = kept, ended
        else:
            out_ref[:bw, columns(p)], out_ref[bw:, columns(p)] = kept, ended

    steps = 2 * (ring - 1)

    def first_sweep(p, carry):
        @pl.when((p >= LAG) & (p - LAG < steps))
        def _():
            second(p - LAG, 0)

        @pl.when(jnp.logical_not(last))
        def _():
            up(0, p).wait_recv()

        @pl.when(first)
        def _():
            window[1, p] = below[0, p]

        @pl.when(inner)
        def _():
            for h in range(2):
                initial(h, p).wait_recv()
            apply(0, p)

        return carry

    def second_sweep(p, carry):
        @pl.when(jnp.logical_not(last))
        def _():
            up(1, p).wait_recv()

        apply(1, p)
        return carry

    lax.fori_loop(0, pieces, first_sweep, 0)
    if steps > pieces - LAG:
        lax.fori_loop(max(pieces - LAG, 0), steps, second, 0)
    build_low(1)
    build_up(1)
    lax.fori_loop(0, pieces, second_sweep, 0)

    for slot, when in ((LOW0, inner), (UP0, inner), (LOW1, slab >= 0), (UP1, inner), (EXTRA, last)):
        for t in range(ring - 1):
            for way in range(2):
                @pl.when(when & sends(way, t))
                def _():
                    hop(way, slot, t, slab).wait_send()

    @pl.when(jnp.logical_not(last))
    def _():
        for k in range(len(moved)):
            shift(k).wait_send()

    def finish(p, carry):
        @pl.when(inner)
        def _():
            up(0, p).wait_send()
            up(1, p).wait_send()

        @pl.when(jnp.logical_not(last))
        def _():
            initial(0, p).wait_send()
            initial(1, p).wait_send()

        return carry

    lax.fori_loop(0, pieces, finish, 0)


def per_device(singular_vectors, reflector_vectors, reflector_factors, sweep_bounds):
    count, ring = lax.axis_size("row"), lax.axis_size("col")
    rows, cols = singular_vectors.shape
    sweeps, blocks, _, span = reflector_vectors.shape
    bw = span // 2
    assert sweeps == 2 and blocks == 2 and rows == span and cols % WIDTH == 0
    pieces = cols // WIDTH
    vmem, dma = pltpu.VMEM, pltpu.SemaphoreType.DMA
    return pl.pallas_call(
        functools.partial(kernel, count, ring),
        out_shape=jax.ShapeDtypeStruct((rows, cols), f32),
        in_specs=[pl.BlockSpec(memory_space=pltpu.SMEM)] + [pl.BlockSpec(memory_space=vmem)] * 3,
        out_specs=pl.BlockSpec(memory_space=vmem),
        scratch_shapes=[
            vmem((5, bw, bw + bw // 2), f32),
            vmem((3, bw // ring, bw + bw // 2), f32),
            vmem((2, span, 3 * bw), bf16), vmem((2, span, 3 * bw), bf16),
            vmem((2, span, span), bf16), vmem((2, span, span), bf16),
            vmem((span, span), bf16), vmem((span, span), bf16),
            vmem((2, pieces, bw, WIDTH), f32),
            vmem((2, pieces, bw, WIDTH), f32),
            vmem((2, pieces, bw, WIDTH), f32),
            dma((3,)), dma((3,)), dma((2, 5, ring)), dma((2, 5, ring)),
            dma((2, pieces)), dma((2, pieces)), dma((2, pieces)), dma((2, pieces)),
        ],
        compiler_params=pltpu.CompilerParams(
            collective_id=0, has_side_effects=True, vmem_limit_bytes=56 * 2**20
        ),
    )(sweep_bounds, singular_vectors, reflector_vectors, reflector_factors)


def solution(mesh):
    placed = (P("row", "col"), P(None, "row", "col", None), P(None, "row", "col", None), P())
    return jax.shard_map(
        per_device, mesh=mesh, in_specs=placed, out_specs=P("row", "col"), check_vma=False
    )
```

time: 108 us -> 81.4 us (0.75)
  Pallas kernels: 105 us -> 78.1 us
    pallas_call x1, Pallas kernels: 105 us -> 78.1 us  [per_device(): pl.pallas_call(functools.partial(kernel, count, ring), out_shape=jax.Shap...]
where the time goes in v2:
time: 81.4 us; the launch traced here: 81.2 us
  Pallas kernels  78.1 us (96%)
  local copies, waits for them, and re-layouts  3.16 us (4%)
    pallas_call x1, Pallas kernels, per_device(): pl.pallas_call(functools.partial(kernel, count, ring), out_shape=jax.Shap...  78.1 us
    unnamed x1, local copies, waits for them, and re-layouts  3.16 us

profile of v2, /device:TPU:0, one launch (start us, length us, event | category | flops | bytes accessed | tf_op | source)
XLA Modules:
  0.0 81.2 jit_solution(8347818993298149311)
XLA Ops:
  0.0 78.1 %shard_map.46 = f32[512,1024]{1,0:T(8,128)} custom-call(s32[2,2]{1,0:T(2,128)} %bounds_ref.1, f32[512,1024]{1,0:T(8,128)} %x_ref.1, f32[2,2,64,512]{3,2,1,0:T(8,128)} %vec_ref.1, f32[2,2,64,256]{3,2,1,0:T(8,128)} %fac_ref.1), custom_call_target="tpu_custom_call" | custom-call | tf_op jit(solution)/shard_map/pallas_call | solution.py:324
  78.1 3.2 %copy.6 = f32[512,1024]{1,0:T(8,128)} copy(f32[512,1024]{1,0:T(8,128)} %shard_map.46) | data formatting | bytes 4194304

commit v3 on v2

--- a/solution.py
+++ b/solution.py
@@ -24,23 +24,26 @@
 
 
 LOW0, UP0, LOW1, UP1, EXTRA = range(5)
-LAG = 2
 
 
 def kernel(
     count, ring, bounds_ref, x_ref, vec_ref, fac_ref, out_ref,
     gathered, outbox, upper_high, upper_low, lower_high, lower_low, extra_high, extra_low,
-    window, below, tops,
-    shift_send, shift_recv, hop_send, hop_recv,
-    first_send, first_recv, up_send, up_recv,
+    cross, crossed, cross_high, cross_low,
+    window, below, tops, partner, nearby, local,
+    shift_send, shift_recv, hop_send, hop_recv, far_send, far_recv, cross_send, cross_recv,
+    first_send, first_recv, up_send, up_recv, over_send, over_recv, near_send, near_recv,
 ):
     me, slab = lax.axis_index("row"), lax.axis_index("col")
     bw = x_ref.shape[0] // 2
     half = bw // 2
     part = bw // ring
-    pieces, width = below.shape[1], below.shape[3]
+    pairs, width = below.shape[1], WIDTH
+    pieces = 2 * pairs
     first, last = me == 0, me == count - 1
     inner = jnp.logical_not(first)
+    odd = lax.rem(me, 2) == 1
+    even = jnp.logical_not(odd)
 
     def block_rows(owner):
         return pl.ds(pl.multiple_of(owner * part, part), part)
@@ -48,6 +51,12 @@
     def columns(p):
         return pl.ds(pl.multiple_of(p * width, width), width)
 
+    def lanes(p):
+        return columns(lax.rem(p, 2))
+
+    def broad(q):
+        return pl.ds(pl.multiple_of(q * 2 * width, 2 * width), 2 * width)
+
     barrier = pltpu.get_barrier_semaphore()
 
     @pl.when(inner)
@@ -58,12 +67,18 @@
     def _():
         pl.semaphore_signal(barrier, inc=1, device_id={"row": me + 1}, device_id_type=MESH)
 
-    for way in range(2):
-        @pl.when(slab + 1 < ring if way == 0 else slab >= 1)
-        def _():
-            pl.semaphore_signal(
-                barrier, inc=1, device_id={"col": slab + (1 - 2 * way)}, device_id_type=MESH
-            )
+    @pl.when(odd & (me > 1))
+    def _():
+        pl.semaphore_signal(barrier, inc=1, device_id={"row": me - 2}, device_id_type=MESH)
+
+    @pl.when(odd & (me + 2 < count))
+    def _():
+        pl.semaphore_signal(barrier, inc=1, device_id={"row": me + 2}, device_id_type=MESH)
+
+    for k in range(1, ring):
+        pl.semaphore_signal(
+            barrier, inc=1, device_id={"col": lax.rem(slab + k, ring)}, device_id_type=MESH
+        )
 
     def stage(rows, s, b):
         w, f = vec_ref[s, b], fac_ref[s, b]
@@ -89,7 +104,8 @@
 
     pl.semaphore_wait(
         barrier,
-        greeted(me > 0) + greeted(me < count - 1) + greeted(slab > 0) + greeted(slab < ring - 1),
+        greeted(me > 0) + greeted(me < count - 1) + ring - 1
+        + greeted(odd & (me > 1)) + greeted(odd & (me + 2 < count)),
     )
 
     def shift(k):
@@ -101,7 +117,7 @@
 
     def initial(h, p):
         return pltpu.make_async_remote_copy(
-            src_ref=x_ref.at[pl.ds(h * bw, bw), columns(p)], dst_ref=window.at[h, p],
+            src_ref=x_ref.at[pl.ds(h * bw, bw), columns(p)], dst_ref=window.at[h, p // 2, :, lanes(p)],
             send_sem=first_send.at[h, p], recv_sem=first_recv.at[h, p],
             device_id={"row": me + 1}, device_id_type=MESH,
         )
@@ -159,13 +175,22 @@
             get_hops(slot, t, when)
             send_hops(slot, t + 1, when)
 
-    send_hops(LOW1, 0, slab >= 0)
+    def far(slot, k, owner):
+        block = gathered.at[slot, block_rows(owner)]
+        return pltpu.make_async_remote_copy(
+            src_ref=block, dst_ref=block,
+            send_sem=far_send.at[slot - LOW1, k], recv_sem=far_recv.at[slot - LOW1, k],
+            device_id={"col": lax.rem(slab + k, ring)}, device_id_type=MESH,
+        )
+
+    for k in range(1, ring):
+        far(LOW1, k, slab).start()
 
     @pl.when(inner)
     def _():
         shift(2).wait_recv()
-
-    send_hops(UP1, 0, inner)
+        for k in range(1, ring):
+            far(UP1, k, slab).start()
 
     def whole(slot, s, block):
         row = lax.broadcasted_iota(jnp.int32, (bw, bw), 0)
@@ -197,16 +222,34 @@
         upper_high[s, :, :bw], upper_low[s, :, :bw] = split(q[:, :bw])
         upper_high[s, :, bw:], upper_low[s, :, bw:] = split(mixed)
 
+        @pl.when(even & inner)
+        def _():
+            cross[s] = mixed[:bw, bw:]
+            across(s).start()
+
+    def across(s):
+        return pltpu.make_async_remote_copy(
+            src_ref=cross.at[s], dst_ref=crossed.at[s],
+            send_sem=cross_send.at[s], recv_sem=cross_recv.at[s],
+            device_id={"row": me + 1}, device_id_type=MESH,
+        )
+
+    def get_across(s):
+        @pl.when(odd & (me > 1))
+        def _():
+            across(s).wait_recv()
+            cross_high[s], cross_low[s] = split(crossed[s])
+
     @pl.when(last)
     def _():
         extra_high[...], extra_low[...] = split(whole(EXTRA, 0, 2 * me))
 
         def own(p, carry):
-            both = dot3((extra_high[...], extra_low[...]), split(x_ref[:, columns(p)]))
+            both = dot3((extra_high[...], extra_low[...]), split(x_ref[:, broad(p)]))
             below[0, p], below[1, p] = both[:bw], both[bw:]
             return carry
 
-        lax.fori_loop(0, pieces, own, 0)
+        lax.fori_loop(0, pairs, own, 0)
 
     @pl.when(inner)
     def _():
@@ -219,89 +262,172 @@
         build_up(0)
 
     def up(s, p):
-        return pltpu.make_async_remote_copy(
-            src_ref=tops.at[s, p], dst_ref=below.at[s, p],
+        block = (s, p // 2, slice(None), lanes(p))
+        return pltpu.make_async_remote_copy(
+            src_ref=tops.at[block], dst_ref=below.at[block],
             send_sem=up_send.at[s, p], recv_sem=up_recv.at[s, p],
+            device_id={"row": me - 2}, device_id_type=MESH,
+        )
+
+    def over(s, p):
+        block = (s, p // 2, slice(None), lanes(p))
+        return pltpu.make_async_remote_copy(
+            src_ref=partner.at[block], dst_ref=below.at[block],
+            send_sem=over_send.at[s, p], recv_sem=over_recv.at[s, p],
             device_id={"row": me - 1}, device_id_type=MESH,
         )
 
-    def second(q, carry):
-        t, slot = q // 2, LOW1 + q % 2
-        when = inner | (slot == LOW1)
-        get_hops(slot, t, when)
-        send_hops(slot, t + 1, when)
-        return carry
-
-    def apply(s, p):
-        parts = split(jnp.concatenate([window[0, p], window[1, p], below[s, p]], axis=0))
-
-        @pl.when(inner)
-        def _():
-            tops[s, p] = dot3((upper_high[s, :bw], upper_low[s, :bw]), parts)
-            up(s, p).start()
-
+    def near(s, q):
+        return pltpu.make_async_remote_copy(
+            src_ref=partner.at[s, q], dst_ref=nearby.at[s, q],
+            send_sem=near_send.at[s, q], recv_sem=near_recv.at[s, q],
+            device_id={"row": me + 1}, device_id_type=MESH,
+        )
+
+    def get_initial(q):
+        for h in range(2):
+            for i in range(2):
+                initial(h, 2 * q + i).wait_recv()
+
+    def share(s, q):
+        parts = split(jnp.concatenate([window[0, q], window[1, q]], axis=0))
+        return dot3((upper_high[s, :bw, :2 * bw], upper_low[s, :bw, :2 * bw]), parts)
+
+    def settle(s, q):
+        parts = split(jnp.concatenate([window[0, q], window[1, q], below[s, q]], axis=0))
+        kept = dot3((upper_high[s, bw:], upper_low[s, bw:]), parts)
         ended = dot3((lower_high[s, bw:], lower_low[s, bw:]), tuple(value[bw:] for value in parts))
-        kept = dot3((upper_high[s, bw:], upper_low[s, bw:]), parts)
         if s == 0:
-            window[0, p], window[1, p] = kept, ended
+            window[0, q], window[1, q] = kept, ended
         else:
-            out_ref[:bw, columns(p)], out_ref[bw:, columns(p)] = kept, ended
-
-    steps = 2 * (ring - 1)
-
-    def first_sweep(p, carry):
-        @pl.when((p >= LAG) & (p - LAG < steps))
-        def _():
-            second(p - LAG, 0)
-
-        @pl.when(jnp.logical_not(last))
-        def _():
-            up(0, p).wait_recv()
-
-        @pl.when(first)
-        def _():
-            window[1, p] = below[0, p]
-
-        @pl.when(inner)
-        def _():
-            for h in range(2):
-                initial(h, p).wait_recv()
-            apply(0, p)
-
-        return carry
-
-    def second_sweep(p, carry):
-        @pl.when(jnp.logical_not(last))
-        def _():
-            up(1, p).wait_recv()
-
-        apply(1, p)
-        return carry
-
-    lax.fori_loop(0, pieces, first_sweep, 0)
-    if steps > pieces - LAG:
-        lax.fori_loop(max(pieces - LAG, 0), steps, second, 0)
+            out_ref[:bw, broad(q)], out_ref[bw:, broad(q)] = kept, ended
+
+    def odd_sweep(s):
+        def pair(q, carry):
+            if s == 0:
+                get_initial(q)
+            local[...] = share(s, q)
+
+            @pl.when(me > 1)
+            def _():
+                near(s, q).wait_recv()
+
+            for i in range(2):
+                p = 2 * q + i
+                half_lanes = slice(i * width, (i + 1) * width)
+
+                @pl.when(jnp.logical_not(last))
+                def _():
+                    up(s, p).wait_recv()
+
+                step = (upper_high[s, :bw, 2 * bw:], upper_low[s, :bw, 2 * bw:])
+                mine = local[:, half_lanes] + dot3(step, split(below[s, q, :, half_lanes]))
+                partner[s, q, :, half_lanes] = mine
+
+                @pl.when(me > 1)
+                def _():
+                    step = (cross_high[s], cross_low[s])
+                    tops[s, q, :, half_lanes] = nearby[s, q, :, half_lanes] + dot3(step, split(mine))
+                    up(s, p).start()
+
+                over(s, p).start()
+
+            settle(s, q)
+            return carry
+
+        lax.fori_loop(0, pairs, pair, 0)
+
+    def even_sweep(s):
+        def pair(q, carry):
+            @pl.when((q < pairs) & inner)
+            def _():
+                if s == 0:
+                    get_initial(q)
+                partner[s, q] = share(s, q)
+                near(s, q).start()
+
+            @pl.when(q >= 1)
+            def _():
+                over(s, 2 * q - 2).wait_recv()
+                over(s, 2 * q - 1).wait_recv()
+                if s == 1:
+                    settle(s, q - 1)
+
+            if s == 0:
+                @pl.when((q >= 1) & inner)
+                def _():
+                    settle(s, q - 1)
+
+                @pl.when((q >= 1) & first)
+                def _():
+                    window[1, q - 1] = below[0, q - 1]
+
+            return carry
+
+        lax.fori_loop(0, pairs + 1, pair, 0)
+
+    def sweep(s):
+        get_across(s)
+
+        @pl.when(odd)
+        def _():
+            odd_sweep(s)
+
+        @pl.when(even)
+        def _():
+            even_sweep(s)
+
+    sweep(0)
+    for k in range(1, ring):
+        far(LOW1, k, lax.rem(slab + ring - k, ring)).wait_recv()
+
+    @pl.when(inner)
+    def _():
+        for k in range(1, ring):
+            far(UP1, k, lax.rem(slab + ring - k, ring)).wait_recv()
+
     build_low(1)
     build_up(1)
-    lax.fori_loop(0, pieces, second_sweep, 0)
-
-    for slot, when in ((LOW0, inner), (UP0, inner), (LOW1, slab >= 0), (UP1, inner), (EXTRA, last)):
+    sweep(1)
+
+    for slot, when in ((LOW0, inner), (UP0, inner), (EXTRA, last)):
         for t in range(ring - 1):
             for way in range(2):
                 @pl.when(when & sends(way, t))
                 def _():
                     hop(way, slot, t, slab).wait_send()
 
+    for k in range(1, ring):
+        far(LOW1, k, slab).wait_send()
+
+    @pl.when(inner)
+    def _():
+        for k in range(1, ring):
+            far(UP1, k, slab).wait_send()
+
     @pl.when(jnp.logical_not(last))
     def _():
         for k in range(len(moved)):
             shift(k).wait_send()
 
+    @pl.when(even & inner)
+    def _():
+        across(0).wait_send()
+        across(1).wait_send()
+
     def finish(p, carry):
-        @pl.when(inner)
-        def _():
-            up(0, p).wait_send()
-            up(1, p).wait_send()
+        for s in range(2):
+            @pl.when(odd & (me > 1))
+            def _():
+                up(s, p).wait_send()
+
+            @pl.when(odd)
+            def _():
+                over(s, p).wait_send()
+
+            @pl.when(even & inner & (p < pairs))
+            def _():
+                near(s, p).wait_send()
 
         @pl.when(jnp.logical_not(last))
         def _():
@@ -318,8 +444,9 @@
     rows, cols = singular_vectors.shape
     sweeps, blocks, _, span = reflector_vectors.shape
     bw = span // 2
-    assert sweeps == 2 and blocks == 2 and rows == span and cols % WIDTH == 0
-    pieces = cols // WIDTH
+    assert sweeps == 2 and blocks == 2 and rows == span and cols % (2 * WIDTH) == 0
+    assert count % 2 == 0
+    pairs = cols // (2 * WIDTH)
     vmem, dma = pltpu.VMEM, pltpu.SemaphoreType.DMA
     return pl.pallas_call(
         functools.partial(kernel, count, ring),
@@ -332,11 +459,18 @@
             vmem((2, span, 3 * bw), bf16), vmem((2, span, 3 * bw), bf16),
             vmem((2, span, span), bf16), vmem((2, span, span), bf16),
             vmem((span, span), bf16), vmem((span, span), bf16),
-            vmem((2, pieces, bw, WIDTH), f32),
-            vmem((2, pieces, bw, WIDTH), f32),
-            vmem((2, pieces, bw, WIDTH), f32),
+            vmem((2, bw, bw), f32), vmem((2, bw, bw), f32),
+            vmem((2, bw, bw), bf16), vmem((2, bw, bw), bf16),
+            vmem((2, pairs, bw, 2 * WIDTH), f32),
+            vmem((2, pairs, bw, 2 * WIDTH), f32),
+            vmem((2, pairs, bw, 2 * WIDTH), f32),
+            vmem((2, pairs, bw, 2 * WIDTH), f32),
+            vmem((2, pairs, bw, 2 * WIDTH), f32),
+            vmem((bw, 2 * WIDTH), f32),
             dma((3,)), dma((3,)), dma((2, 5, ring)), dma((2, 5, ring)),
-            dma((2, pieces)), dma((2, pieces)), dma((2, pieces)), dma((2, pieces)),
+            dma((2, ring)), dma((2, ring)), dma((2,)), dma((2,)),
+            dma((2, 2 * pairs)), dma((2, 2 * pairs)), dma((2, 2 * pairs)), dma((2, 2 * pairs)),
+            dma((2, 2 * pairs)), dma((2, 2 * pairs)), dma((2, pairs)), dma((2, pairs)),
         ],
         compiler_params=pltpu.CompilerParams(
             collective_id=0, has_side_effects=True, vmem_limit_bytes=56 * 2**20

time: 81.4 us -> 82.6 us (1.015)
  Pallas kernels: 78.1 us -> 79.3 us
    pallas_call x1, Pallas kernels: 78.1 us -> 79.3 us  [per_device(): pl.pallas_call(functools.partial(kernel, count, ring), out_shape=jax.Shap...]
where the time goes in v3:
time: 82.6 us; the launch traced here: 82.4 us
  Pallas kernels  79.3 us (96%)
  local copies, waits for them, and re-layouts  3.16 us (4%)
    pallas_call x1, Pallas kernels, per_device(): pl.pallas_call(functools.partial(kernel, count, ring), out_shape=jax.Shap...  79.3 us
    unnamed x1, local copies, waits for them, and re-layouts  3.16 us

profile of v3, /device:TPU:0, one launch (start us, length us, event | category | flops | bytes accessed | tf_op | source)
XLA Modules:
  0.0 82.4 jit_solution(11634060768717528895)
XLA Ops:
  0.0 79.3 %shard_map.46 = f32[512,1024]{1,0:T(8,128)} custom-call(s32[2,2]{1,0:T(2,128)} %bounds_ref.1, f32[512,1024]{1,0:T(8,128)} %x_ref.1, f32[2,2,64,512]{3,2,1,0:T(8,128)} %vec_ref.1, f32[2,2,64,256]{3,2,1,0:T(8,128)} %fac_ref.1), custom_call_target="tpu_custom_call" | custom-call | tf_op jit(solution)/shard_map/pallas_call | solution.py:451
  79.3 3.2 %copy.6 = f32[512,1024]{1,0:T(8,128)} copy(f32[512,1024]{1,0:T(8,128)} %shard_map.46) | data formatting | bytes 4194304

commit v4 on v3

--- a/solution.py
+++ b/solution.py
@@ -19,24 +19,25 @@
 
 def dot3(a, b):
     (a_high, a_low), (b_high, b_low) = a, b
-    dot = functools.partial(jnp.dot, preferred_element_type=f32)
-    return dot(a_high, b_high) + (dot(a_high, b_low) + dot(a_low, b_high))
-
-
+    left = jnp.concatenate([a_high, a_low, a_high], axis=1)
+    right = jnp.concatenate([b_high, b_high, b_low], axis=0)
+    return jnp.dot(left, right, preferred_element_type=f32)
+
+
+NEAR = 64
 LOW0, UP0, LOW1, UP1, EXTRA = range(5)
 
 
 def kernel(
     count, ring, bounds_ref, x_ref, vec_ref, fac_ref, out_ref,
-    gathered, outbox, upper_high, upper_low, lower_high, lower_low, extra_high, extra_low,
+    wide, narrow, wide_box, narrow_box, upper_high, upper_low, lower_high, lower_low, extra_high, extra_low,
     cross, crossed, cross_high, cross_low,
     window, below, tops, partner, nearby, local,
-    shift_send, shift_recv, hop_send, hop_recv, far_send, far_recv, cross_send, cross_recv,
+    shift_send, shift_recv, hop_send, hop_recv, cross_send, cross_recv,
     first_send, first_recv, up_send, up_recv, over_send, over_recv, near_send, near_recv,
 ):
     me, slab = lax.axis_index("row"), lax.axis_index("col")
     bw = x_ref.shape[0] // 2
-    half = bw // 2
     part = bw // ring
     pairs, width = below.shape[1], WIDTH
     pieces = 2 * pairs
@@ -44,6 +45,7 @@
     inner = jnp.logical_not(first)
     odd = lax.rem(me, 2) == 1
     even = jnp.logical_not(odd)
+    early = me >= count - 4
 
     def block_rows(owner):
         return pl.ds(pl.multiple_of(owner * part, part), part)
@@ -75,28 +77,40 @@
     def _():
         pl.semaphore_signal(barrier, inc=1, device_id={"row": me + 2}, device_id_type=MESH)
 
-    for k in range(1, ring):
-        pl.semaphore_signal(
-            barrier, inc=1, device_id={"col": lax.rem(slab + k, ring)}, device_id_type=MESH
-        )
-
-    def stage(rows, s, b):
-        w, f = vec_ref[s, b], fac_ref[s, b]
-        rows[:, :bw] = w[:, :bw] + w[:, bw:]
-        rows[:, bw:] = jnp.where(slab * part < half, f[:, :half], f[:, half:])
-
-    moved = ((LOW0, 0, 1), (UP0, 0, 0), (UP1, 1, 1))
-    for k, (slot, s, b) in enumerate(moved):
-        stage(outbox.at[k], s, b)
-    stage(gathered.at[LOW1, block_rows(slab)], 1, 0)
+    for way in range(2):
+        @pl.when(slab + 1 < ring if way == 0 else slab >= 1)
+        def _():
+            pl.semaphore_signal(
+                barrier, inc=1, device_id={"col": slab + (1 - 2 * way)}, device_id_type=MESH
+            )
+
+    def triangles(s, b):
+        w = vec_ref[s, b]
+        return w[:, :bw] + w[:, bw:]
+
+    def diagonal(s, b):
+        f = fac_ref[s, b]
+        return sum(
+            jnp.where(slab * part // NEAR == k, f[:, k * NEAR:(k + 1) * NEAR], 0.0)
+            for k in range(bw // NEAR)
+        )
+
+    mine = block_rows(slab)
+    narrow_box[...] = triangles(0, 0)
+    wide_box[0, :, :bw], wide_box[1, :, :bw] = triangles(0, 1), triangles(1, 1)
+    wide_box[0, :, bw:] = jnp.concatenate([diagonal(0, 1), diagonal(0, 0)], axis=1)
+    wide_box[1, :, bw:] = jnp.concatenate([diagonal(1, 0), diagonal(1, 1)], axis=1)
+    narrow[1, mine] = triangles(1, 0)
 
     @pl.when(last)
     def _():
-        stage(gathered.at[EXTRA, block_rows(slab)], 0, 0)
+        wide[2, mine, :bw] = triangles(0, 0)
+        wide[2, mine, bw:] = jnp.concatenate([diagonal(0, 0)] * 2, axis=1)
 
     @pl.when(first)
     def _():
-        gathered[UP1] = jnp.zeros((bw, bw + half), f32)
+        wide[1, mine, :bw] = jnp.zeros((part, bw), f32)
+        wide[1, mine, bw:] = jnp.concatenate([diagonal(1, 0)] * 2, axis=1)
         window[0] = jnp.zeros_like(window[0])
 
     def greeted(there):
@@ -104,13 +118,17 @@
 
     pl.semaphore_wait(
         barrier,
-        greeted(me > 0) + greeted(me < count - 1) + ring - 1
+        greeted(me > 0) + greeted(me < count - 1) + greeted(slab > 0) + greeted(slab < ring - 1)
         + greeted(odd & (me > 1)) + greeted(odd & (me + 2 < count)),
     )
 
+    place = {LOW0: wide.at[0], UP0: narrow.at[0], LOW1: narrow.at[1], UP1: wide.at[1], EXTRA: wide.at[2]}
+    moved = ((LOW0, wide_box.at[0]), (UP0, narrow_box), (UP1, wide_box.at[1]))
+
     def shift(k):
-        return pltpu.make_async_remote_copy(
-            src_ref=outbox.at[k], dst_ref=gathered.at[moved[k][0], block_rows(slab)],
+        slot, box = moved[k]
+        return pltpu.make_async_remote_copy(
+            src_ref=box, dst_ref=place[slot].at[mine],
             send_sem=shift_send.at[k], recv_sem=shift_recv.at[k],
             device_id={"row": me + 1}, device_id_type=MESH,
         )
@@ -123,7 +141,7 @@
         )
 
     def hop(way, slot, t, owner):
-        block = gathered.at[slot, block_rows(owner)]
+        block = place[slot].at[block_rows(owner)]
         return pltpu.make_async_remote_copy(
             src_ref=block, dst_ref=block,
             send_sem=hop_send.at[way, slot, t], recv_sem=hop_recv.at[way, slot, t],
@@ -175,22 +193,22 @@
             get_hops(slot, t, when)
             send_hops(slot, t + 1, when)
 
-    def far(slot, k, owner):
-        block = gathered.at[slot, block_rows(owner)]
-        return pltpu.make_async_remote_copy(
-            src_ref=block, dst_ref=block,
-            send_sem=far_send.at[slot - LOW1, k], recv_sem=far_recv.at[slot - LOW1, k],
-            device_id={"col": lax.rem(slab + k, ring)}, device_id_type=MESH,
-        )
-
-    for k in range(1, ring):
-        far(LOW1, k, slab).start()
+    always = slab >= 0
+    send_hops(LOW1, 0, always)
 
     @pl.when(inner)
     def _():
         shift(2).wait_recv()
-        for k in range(1, ring):
-            far(UP1, k, slab).start()
+        both = wide[1, mine, bw:]
+        lane = lax.broadcasted_iota(jnp.int32, both.shape, 1)
+        wide[1, mine, bw:] = jnp.where(lane < NEAR, wide_box[1, :, bw:], both)
+
+    send_hops(UP1, 0, always)
+
+    def second(k):
+        t, slot = k // 2, (LOW1, UP1)[k % 2]
+        get_hops(slot, t, always)
+        send_hops(slot, t + 1, always)
 
     def whole(slot, s, block):
         row = lax.broadcasted_iota(jnp.int32, (bw, bw), 0)
@@ -200,18 +218,31 @@
         unit = jnp.where(row2 == col2, 1.0, 0.0).astype(f32)
         start = block * bw
         live = (start >= bounds_ref[s, 0]) & (start <= bounds_ref[s, 1])
-        packed = gathered[slot, :, :bw]
-        factor = gathered[slot, :, bw:] * jnp.where(live, 1.0, 0.0).astype(f32)
+        packed = place[slot][:, :bw]
+        near = place[EXTRA if slot == EXTRA else (LOW0, UP1)[s]][:, bw:]
+        if slot in (UP0, UP1):
+            near = near[:, NEAR:]
+        else:
+            near = near[:, :NEAR]
+        near = near * jnp.where(live, 1.0, 0.0).astype(f32)
         w = jnp.concatenate(
             [jnp.where(col >= row, packed, 0.0), jnp.where(col < row, packed, 0.0)], axis=1
         )
         w_high, w_low = split(w)
-        head, tail = (w_high[:half], w_low[:half]), (w_high[half:], w_low[half:])
-        g_tail = dot3(split(factor[half:]), tail)
-        u = dot3(head, tuple(value.T for value in tail))
-        g_head = dot3(split(factor[:half]), split(w[:half] - dot3(split(u), split(g_tail))))
-        g = jnp.concatenate([g_head, g_tail], axis=0)
-        return unit - dot3((w_high.T, w_low.T), split(g))
+        turned = (w_high.T, w_low.T)
+        gram = dot3((w_high, w_low), turned)
+        factor = jnp.where(
+            row // NEAR == col // NEAR, jnp.concatenate([near] * (bw // NEAR), axis=1), 0.0
+        )
+        size = NEAR
+        while size < bw:
+            cross_part = (row // (2 * size) == col // (2 * size)) & (row // size < col // size)
+            parts = split(factor)
+            right = dot3(split(jnp.where(cross_part, gram, 0.0)), parts)
+            factor = factor - dot3(parts, split(right))
+            size *= 2
+        g = dot3(split(factor), (w_high, w_low))
+        return unit - dot3(turned, split(g))
 
     def build_low(s):
         lower_high[s], lower_low[s] = split(whole(2 * s, s, 2 * me - 1 + s))
@@ -261,6 +292,15 @@
     def _():
         build_up(0)
 
+    steps = 2 * (ring - 1)
+
+    @pl.when(jnp.logical_not(early))
+    def _():
+        for k in range(steps):
+            second(k)
+        build_low(1)
+        build_up(1)
+
     def up(s, p):
         block = (s, p // 2, slice(None), lanes(p))
         return pltpu.make_async_remote_copy(
@@ -288,6 +328,12 @@
         for h in range(2):
             for i in range(2):
                 initial(h, 2 * q + i).wait_recv()
+
+    def second_at(p):
+        for k in range(min(steps, pieces - 2)):
+            @pl.when(early & (p == k + 1))
+            def _():
+                second(k)
 
     def share(s, q):
         parts = split(jnp.concatenate([window[0, q], window[1, q]], axis=0))
@@ -331,6 +377,8 @@
                     up(s, p).start()
 
                 over(s, p).start()
+                if s == 0:
+                    second_at(p)
 
             settle(s, q)
             return carry
@@ -346,6 +394,10 @@
                 partner[s, q] = share(s, q)
                 near(s, q).start()
 
+            if s == 0:
+                second_at(2 * q - 1)
+                second_at(2 * q)
+
             @pl.when(q >= 1)
             def _():
                 over(s, 2 * q - 2).wait_recv()
@@ -378,32 +430,22 @@
             even_sweep(s)
 
     sweep(0)
-    for k in range(1, ring):
-        far(LOW1, k, lax.rem(slab + ring - k, ring)).wait_recv()
-
-    @pl.when(inner)
-    def _():
-        for k in range(1, ring):
-            far(UP1, k, lax.rem(slab + ring - k, ring)).wait_recv()
-
-    build_low(1)
-    build_up(1)
+
+    @pl.when(early)
+    def _():
+        for k in range(min(steps, pieces - 2), steps):
+            second(k)
+        build_low(1)
+        build_up(1)
+
     sweep(1)
 
-    for slot, when in ((LOW0, inner), (UP0, inner), (EXTRA, last)):
+    for slot, when in ((LOW0, inner), (UP0, inner), (LOW1, always), (UP1, always), (EXTRA, last)):
         for t in range(ring - 1):
             for way in range(2):
                 @pl.when(when & sends(way, t))
                 def _():
                     hop(way, slot, t, slab).wait_send()
-
-    for k in range(1, ring):
-        far(LOW1, k, slab).wait_send()
-
-    @pl.when(inner)
-    def _():
-        for k in range(1, ring):
-            far(UP1, k, slab).wait_send()
 
     @pl.when(jnp.logical_not(last))
     def _():
@@ -454,8 +496,8 @@
         in_specs=[pl.BlockSpec(memory_space=pltpu.SMEM)] + [pl.BlockSpec(memory_space=vmem)] * 3,
         out_specs=pl.BlockSpec(memory_space=vmem),
         scratch_shapes=[
-            vmem((5, bw, bw + bw // 2), f32),
-            vmem((3, bw // ring, bw + bw // 2), f32),
+            vmem((3, bw, bw + 2 * NEAR), f32), vmem((2, bw, bw), f32),
+            vmem((2, bw // ring, bw + 2 * NEAR), f32), vmem((bw // ring, bw), f32),
             vmem((2, span, 3 * bw), bf16), vmem((2, span, 3 * bw), bf16),
             vmem((2, span, span), bf16), vmem((2, span, span), bf16),
             vmem((span, span), bf16), vmem((span, span), bf16),
@@ -468,7 +510,7 @@
             vmem((2, pairs, bw, 2 * WIDTH), f32),
             vmem((bw, 2 * WIDTH), f32),
             dma((3,)), dma((3,)), dma((2, 5, ring)), dma((2, 5, ring)),
-            dma((2, ring)), dma((2, ring)), dma((2,)), dma((2,)),
+            dma((2,)), dma((2,)),
             dma((2, 2 * pairs)), dma((2, 2 * pairs)), dma((2, 2 * pairs)), dma((2, 2 * pairs)),
             dma((2, 2 * pairs)), dma((2, 2 * pairs)), dma((2, pairs)), dma((2, pairs)),
         ],

time: 82.6 us -> 81 us (0.981)
  Pallas kernels: 79.3 us -> 77.6 us
    pallas_call x1, Pallas kernels: 79.3 us -> 77.6 us  [per_device(): pl.pallas_call(functools.partial(kernel, count, ring), out_shape=jax.Shap...]
where the time goes in v4:
time: 81 us; the launch traced here: 80.8 us
  Pallas kernels  77.6 us (96%)
  local copies, waits for them, and re-layouts  3.16 us (4%)
    pallas_call x1, Pallas kernels, per_device(): pl.pallas_call(functools.partial(kernel, count, ring), out_shape=jax.Shap...  77.6 us
    unnamed x1, local copies, waits for them, and re-layouts  3.16 us

profile of v4, /device:TPU:0, one launch (start us, length us, event | category | flops | bytes accessed | tf_op | source)
XLA Modules:
  0.0 80.8 jit_solution(17804103529635683689)
XLA Ops:
  0.0 77.6 %shard_map.46 = f32[512,1024]{1,0:T(8,128)} custom-call(s32[2,2]{1,0:T(2,128)} %bounds_ref.1, f32[512,1024]{1,0:T(8,128)} %x_ref.1, f32[2,2,64,512]{3,2,1,0:T(8,128)} %vec_ref.1, f32[2,2,64,256]{3,2,1,0:T(8,128)} %fac_ref.1), custom_call_target="tpu_custom_call" | custom-call | tf_op jit(solution)/shard_map/pallas_call | solution.py:493
  77.6 3.2 %copy.6 = f32[512,1024]{1,0:T(8,128)} copy(f32[512,1024]{1,0:T(8,128)} %shard_map.46) | data formatting | bytes 4194304

commit v5 on v4

--- a/solution.py
+++ b/solution.py
@@ -38,6 +38,7 @@
 ):
     me, slab = lax.axis_index("row"), lax.axis_index("col")
     bw = x_ref.shape[0] // 2
+    half = bw // 2
     part = bw // ring
     pairs, width = below.shape[1], WIDTH
     pieces = 2 * pairs
@@ -185,10 +186,8 @@
 
         send_hops(slot, 0, inner)
 
-    for t in range(ring - 1):
+    for t in range(ring - 2):
         for slot in (EXTRA, LOW0, UP0):
-            if t == ring - 2 and slot == UP0:
-                break
             when = last if slot == EXTRA else inner
             get_hops(slot, t, when)
             send_hops(slot, t + 1, when)
@@ -210,7 +209,7 @@
         get_hops(slot, t, always)
         send_hops(slot, t + 1, always)
 
-    def whole(slot, s, block):
+    def stages(slot, s, block):
         row = lax.broadcasted_iota(jnp.int32, (bw, bw), 0)
         col = lax.broadcasted_iota(jnp.int32, (bw, bw), 1)
         row2 = lax.broadcasted_iota(jnp.int32, (2 * bw, 2 * bw), 0)
@@ -230,26 +229,52 @@
         )
         w_high, w_low = split(w)
         turned = (w_high.T, w_low.T)
-        gram = dot3((w_high, w_low), turned)
-        factor = jnp.where(
-            row // NEAR == col // NEAR, jnp.concatenate([near] * (bw // NEAR), axis=1), 0.0
-        )
-        size = NEAR
-        while size < bw:
-            cross_part = (row // (2 * size) == col // (2 * size)) & (row // size < col // size)
-            parts = split(factor)
-            right = dot3(split(jnp.where(cross_part, gram, 0.0)), parts)
-            factor = factor - dot3(parts, split(right))
-            size *= 2
-        g = dot3(split(factor), (w_high, w_low))
+        yield
+        gram = dot3((w_high[:bw - NEAR], w_low[:bw - NEAR]), turned)
+        yield
+        wide_near = jnp.concatenate([near] * (bw // NEAR), axis=1)
+        factor = jnp.where(row // NEAR == col // NEAR, wide_near, 0.0)
+        upper, lower = slice(0, NEAR), slice(half, half + NEAR)
+        beside = jnp.concatenate([gram[upper], gram[lower]], axis=0)
+        near_row, near_col = row[:half] // NEAR, col[:half] // NEAR
+        beside = jnp.where(near_col == 2 * near_row + 1, beside, 0.0)
+        right = dot3(split(beside), split(factor))
+        yield
+        outer = jnp.concatenate([wide_near[upper], wide_near[lower]], axis=0)[:, :half]
+        outer = jnp.where(near_row[:, :half] == near_col[:, :half], outer, 0.0)
+        change = dot3(split(outer), split(right))
+        yield
+        nothing = jnp.zeros((NEAR, bw), f32)
+        factor = factor - jnp.concatenate(
+            [change[:NEAR], nothing, change[NEAR:], nothing], axis=0
+        )
+        g_tail = dot3(split(factor[half:, half:]), (w_high[half:], w_low[half:]))
+        yield
+        rest = w[:half] - dot3(split(gram[:half, half:]), split(g_tail))
+        yield
+        g_head = dot3(split(factor[:half, :half]), split(rest))
+        yield
+        g = jnp.concatenate([g_head, g_tail], axis=0)
         return unit - dot3(turned, split(g))
 
-    def build_low(s):
-        lower_high[s], lower_low[s] = split(whole(2 * s, s, 2 * me - 1 + s))
-
-    def build_up(s):
-        q = whole(2 * s + 1, s, 2 * me - 2 + s)
-        mixed = dot3(split(q[:, bw:]), (lower_high[s, :bw], lower_low[s, :bw]))
+    def in_step(*blocks):
+        results = [None] * len(blocks)
+        waiting = list(enumerate(blocks))
+        while waiting:
+            for item in tuple(waiting):
+                try:
+                    next(item[1])
+                except StopIteration as end:
+                    results[item[0]] = end.value
+                    waiting.remove(item)
+        return results
+
+    def build(s):
+        q_low, q = in_step(
+            stages((LOW0, LOW1)[s], s, 2 * me - 1 + s), stages((UP0, UP1)[s], s, 2 * me - 2 + s)
+        )
+        lower_high[s], lower_low[s] = split(q_low[bw:])
+        mixed = dot3(split(q[:, bw:]), split(q_low[:bw]))
         upper_high[s, :, :bw], upper_low[s, :, :bw] = split(q[:, :bw])
         upper_high[s, :, bw:], upper_low[s, :, bw:] = split(mixed)
 
@@ -271,9 +296,11 @@
             across(s).wait_recv()
             cross_high[s], cross_low[s] = split(crossed[s])
 
+    get_hops(EXTRA, ring - 2, last)
+
     @pl.when(last)
     def _():
-        extra_high[...], extra_low[...] = split(whole(EXTRA, 0, 2 * me))
+        extra_high[...], extra_low[...] = split(in_step(stages(EXTRA, 0, 2 * me))[0])
 
         def own(p, carry):
             both = dot3((extra_high[...], extra_low[...]), split(x_ref[:, broad(p)]))
@@ -282,15 +309,13 @@
 
         lax.fori_loop(0, pairs, own, 0)
 
+    get_hops(LOW0, ring - 2, inner)
+
+    get_hops(UP0, ring - 2, inner)
+
     @pl.when(inner)
     def _():
-        build_low(0)
-
-    get_hops(UP0, ring - 2, inner)
-
-    @pl.when(inner)
-    def _():
-        build_up(0)
+        build(0)
 
     steps = 2 * (ring - 1)
 
@@ -298,8 +323,7 @@
     def _():
         for k in range(steps):
             second(k)
-        build_low(1)
-        build_up(1)
+        build(1)
 
     def up(s, p):
         block = (s, p // 2, slice(None), lanes(p))
@@ -342,7 +366,7 @@
     def settle(s, q):
         parts = split(jnp.concatenate([window[0, q], window[1, q], below[s, q]], axis=0))
         kept = dot3((upper_high[s, bw:], upper_low[s, bw:]), parts)
-        ended = dot3((lower_high[s, bw:], lower_low[s, bw:]), tuple(value[bw:] for value in parts))
+        ended = dot3((lower_high[s], lower_low[s]), tuple(value[bw:] for value in parts))
         if s == 0:
             window[0, q], window[1, q] = kept, ended
         else:
@@ -435,8 +459,7 @@
     def _():
         for k in range(min(steps, pieces - 2), steps):
             second(k)
-        build_low(1)
-        build_up(1)
+        build(1)
 
     sweep(1)
 
@@ -487,7 +510,7 @@
     sweeps, blocks, _, span = reflector_vectors.shape
     bw = span // 2
     assert sweeps == 2 and blocks == 2 and rows == span and cols % (2 * WIDTH) == 0
-    assert count % 2 == 0
+    assert count % 2 == 0 and bw == 4 * NEAR and ring >= 2
     pairs = cols // (2 * WIDTH)
     vmem, dma = pltpu.VMEM, pltpu.SemaphoreType.DMA
     return pl.pallas_call(
@@ -499,7 +522,7 @@
             vmem((3, bw, bw + 2 * NEAR), f32), vmem((2, bw, bw), f32),
             vmem((2, bw // ring, bw + 2 * NEAR), f32), vmem((bw // ring, bw), f32),
             vmem((2, span, 3 * bw), bf16), vmem((2, span, 3 * bw), bf16),
-            vmem((2, span, span), bf16), vmem((2, span, span), bf16),
+            vmem((2, bw, span), bf16), vmem((2, bw, span), bf16),
             vmem((span, span), bf16), vmem((span, span), bf16),
             vmem((2, bw, bw), f32), vmem((2, bw, bw), f32),
             vmem((2, bw, bw), bf16), vmem((2, bw, bw), bf16),

time: 81 us -> 75.9 us (0.937)
  Pallas kernels: 77.6 us -> 72.5 us
    pallas_call x1, Pallas kernels: 77.6 us -> 72.5 us  [per_device(): pl.pallas_call(functools.partial(kernel, count, ring), out_shape=jax.Shap...]
where the time goes in v5:
time: 75.9 us; the launch traced here: 75.7 us
  Pallas kernels  72.5 us (96%)
  local copies, waits for them, and re-layouts  3.16 us (4%)
    pallas_call x1, Pallas kernels, per_device(): pl.pallas_call(functools.partial(kernel, count, ring), out_shape=jax.Shap...  72.5 us
    unnamed x1, local copies, waits for them, and re-layouts  3.16 us

profile of v5, /device:TPU:0, one launch (start us, length us, event | category | flops | bytes accessed | tf_op | source)
XLA Modules:
  0.0 75.7 jit_solution(13277999837588752326)
XLA Ops:
  0.0 72.5 %shard_map.46 = f32[512,1024]{1,0:T(8,128)} custom-call(s32[2,2]{1,0:T(2,128)} %bounds_ref.1, f32[512,1024]{1,0:T(8,128)} %x_ref.1, f32[2,2,64,512]{3,2,1,0:T(8,128)} %vec_ref.1, f32[2,2,64,256]{3,2,1,0:T(8,128)} %fac_ref.1), custom_call_target="tpu_custom_call" | custom-call | tf_op jit(solution)/shard_map/pallas_call | solution.py:516
  72.5 3.2 %copy.6 = f32[512,1024]{1,0:T(8,128)} copy(f32[512,1024]{1,0:T(8,128)} %shard_map.46) | data formatting | bytes 4194304

commit v6 on v5

--- a/solution.py
+++ b/solution.py
@@ -29,7 +29,8 @@
 
 
 def kernel(
-    count, ring, bounds_ref, x_ref, vec_ref, fac_ref, out_ref,
+    count, ring, bounds_ref, x_hbm, vec_hbm, fac_hbm, out_ref,
+    x_ref, vec_ref, fac_ref, load,
     wide, narrow, wide_box, narrow_box, upper_high, upper_low, lower_high, lower_low, extra_high, extra_low,
     cross, crossed, cross_high, cross_low,
     window, below, tops, partner, nearby, local,
@@ -46,7 +47,8 @@
     inner = jnp.logical_not(first)
     odd = lax.rem(me, 2) == 1
     even = jnp.logical_not(odd)
-    early = me >= count - 4
+    early = me >= count - 2
+    ahead = me < count - 4
 
     def block_rows(owner):
         return pl.ds(pl.multiple_of(owner * part, part), part)
@@ -59,6 +61,15 @@
 
     def broad(q):
         return pl.ds(pl.multiple_of(q * 2 * width, 2 * width), 2 * width)
+
+    loads = [
+        pltpu.make_async_copy(source, target, load.at[k])
+        for k, (source, target) in enumerate(
+            ((vec_hbm, vec_ref), (fac_hbm, fac_ref), (x_hbm, x_ref))
+        )
+    ]
+    for copy in loads:
+        copy.start()
 
     barrier = pltpu.get_barrier_semaphore()
 
@@ -96,6 +107,8 @@
             for k in range(bw // NEAR)
         )
 
+    loads[0].wait()
+    loads[1].wait()
     mine = block_rows(slab)
     narrow_box[...] = triangles(0, 0)
     wide_box[0, :, :bw], wide_box[1, :, :bw] = triangles(0, 1), triangles(1, 1)
@@ -170,6 +183,7 @@
                 hop(way, slot, t, slab - (1 - 2 * way) * (t + 1)).wait_recv()
 
     send_hops(EXTRA, 0, last)
+    loads[2].wait()
 
     @pl.when(jnp.logical_not(last))
     def _():
@@ -290,39 +304,37 @@
             device_id={"row": me + 1}, device_id_type=MESH,
         )
 
-    def get_across(s):
-        @pl.when(odd & (me > 1))
-        def _():
-            across(s).wait_recv()
-            cross_high[s], cross_low[s] = split(crossed[s])
-
     get_hops(EXTRA, ring - 2, last)
 
     @pl.when(last)
     def _():
         extra_high[...], extra_low[...] = split(in_step(stages(EXTRA, 0, 2 * me))[0])
 
-        def own(p, carry):
-            both = dot3((extra_high[...], extra_low[...]), split(x_ref[:, broad(p)]))
-            below[0, p], below[1, p] = both[:bw], both[bw:]
-            return carry
-
-        lax.fori_loop(0, pairs, own, 0)
+    def own(q):
+        both = dot3((extra_high[...], extra_low[...]), split(x_ref[:, broad(q)]))
+        below[0, q], below[1, q] = both[:bw], both[bw:]
 
     get_hops(LOW0, ring - 2, inner)
 
     get_hops(UP0, ring - 2, inner)
+    steps = 2 * (ring - 1)
+
+    @pl.when(jnp.logical_not(early))
+    def _():
+        for k in range(steps - 2):
+            second(k)
 
     @pl.when(inner)
     def _():
         build(0)
 
-    steps = 2 * (ring - 1)
-
-    @pl.when(jnp.logical_not(early))
-    def _():
-        for k in range(steps):
+    @pl.when(ahead)
+    def _():
+        for k in range(steps - 2, steps):
             second(k)
+
+    @pl.when(ahead)
+    def _():
         build(1)
 
     def up(s, p):
@@ -353,11 +365,32 @@
             for i in range(2):
                 initial(h, 2 * q + i).wait_recv()
 
-    def second_at(p):
-        for k in range(min(steps, pieces - 2)):
-            @pl.when(early & (p == k + 1))
-            def _():
+    odd_places = ((0, 0), (0, 1), (1, 0), (1, 1), (2, 1))
+    even_places = ((1, 1), (2, 1), (3, 0), (3, 0), (3, 0))
+    placed = min(steps - 1, len(odd_places)) if pairs >= 4 else 0
+
+    def build_at(q, when):
+        @pl.when((q == pairs - 1) & early & when)
+        def _():
+            for k in range(placed + 1, steps):
                 second(k)
+
+        @pl.when((q == pairs - 1) & when)
+        def _():
+            build(1)
+
+    def second_at(places, q, place):
+        for k in range(2):
+            @pl.when(jnp.logical_not(early | ahead) & (q == places[k][0]))
+            def _():
+                if places[k][1] == place:
+                    second(steps - 2 + k)
+
+        for k in range(placed):
+            if places[k][1] == place:
+                @pl.when(early & (q == places[k][0]))
+                def _():
+                    second(k + 1)
 
     def share(s, q):
         parts = split(jnp.concatenate([window[0, q], window[1, q]], axis=0))
@@ -372,45 +405,72 @@
         else:
             out_ref[:bw, broad(q)], out_ref[bw:, broad(q)] = kept, ended
 
+    def carries(s, q, half_lanes):
+        step = (upper_high[s, :bw, 2 * bw:], upper_low[s, :bw, 2 * bw:])
+        partner[s, q, :, half_lanes] = local[:, half_lanes] + dot3(
+            step, split(below[s, q, :, half_lanes])
+        )
+
+    def leaving(s, q, half_lanes):
+        onward = dot3((cross_high[s], cross_low[s]), split(partner[s, q, :, half_lanes]))
+        tops[s, q, :, half_lanes] = nearby[s, q, :, half_lanes] + onward
+
     def odd_sweep(s):
         def pair(q, carry):
             if s == 0:
                 get_initial(q)
             local[...] = share(s, q)
 
-            @pl.when(me > 1)
-            def _():
+            @pl.when((q == 0) & (me > 1))
+            def _():
+                across(s).wait_recv()
+                cross_high[s], cross_low[s] = split(crossed[s])
+
+            @pl.when(last)
+            def _():
+                if s == 0:
+                    own(q)
+                carries(s, q, slice(None))
                 near(s, q).wait_recv()
-
-            for i in range(2):
-                p = 2 * q + i
-                half_lanes = slice(i * width, (i + 1) * width)
-
-                @pl.when(jnp.logical_not(last))
-                def _():
+                leaving(s, q, slice(None))
+                for i in range(2):
+                    up(s, 2 * q + i).start()
+                    over(s, 2 * q + i).start()
+
+            @pl.when((me > 1) & jnp.logical_not(last))
+            def _():
+                near(s, q).wait_recv()
+
+            @pl.when(jnp.logical_not(last))
+            def _():
+                for i in range(2):
+                    p = 2 * q + i
+                    half_lanes = slice(i * width, (i + 1) * width)
                     up(s, p).wait_recv()
-
-                step = (upper_high[s, :bw, 2 * bw:], upper_low[s, :bw, 2 * bw:])
-                mine = local[:, half_lanes] + dot3(step, split(below[s, q, :, half_lanes]))
-                partner[s, q, :, half_lanes] = mine
-
-                @pl.when(me > 1)
-                def _():
-                    step = (cross_high[s], cross_low[s])
-                    tops[s, q, :, half_lanes] = nearby[s, q, :, half_lanes] + dot3(step, split(mine))
-                    up(s, p).start()
-
-                over(s, p).start()
-                if s == 0:
-                    second_at(p)
-
+                    carries(s, q, half_lanes)
+
+                    @pl.when(me > 1)
+                    def _():
+                        leaving(s, q, half_lanes)
+                        up(s, p).start()
+
+                    over(s, p).start()
+
+            if s == 0:
+                second_at(odd_places, q, 0)
+                build_at(q, jnp.logical_not(ahead))
             settle(s, q)
+            if s == 0:
+                second_at(odd_places, q, 1)
             return carry
 
         lax.fori_loop(0, pairs, pair, 0)
 
     def even_sweep(s):
         def pair(q, carry):
+            if s == 0:
+                second_at(even_places, q, 0)
+
             @pl.when((q < pairs) & inner)
             def _():
                 if s == 0:
@@ -419,8 +479,8 @@
                 near(s, q).start()
 
             if s == 0:
-                second_at(2 * q - 1)
-                second_at(2 * q)
+                second_at(even_places, q, 1)
+                build_at(q, jnp.logical_not(ahead))
 
             @pl.when(q >= 1)
             def _():
@@ -443,8 +503,6 @@
         lax.fori_loop(0, pairs + 1, pair, 0)
 
     def sweep(s):
-        get_across(s)
-
         @pl.when(odd)
         def _():
             odd_sweep(s)
@@ -453,14 +511,11 @@
         def _():
             even_sweep(s)
 
+    @pl.when(early)
+    def _():
+        second(0)
+
     sweep(0)
-
-    @pl.when(early)
-    def _():
-        for k in range(min(steps, pieces - 2), steps):
-            second(k)
-        build(1)
-
     sweep(1)
 
     for slot, when in ((LOW0, inner), (UP0, inner), (LOW1, always), (UP1, always), (EXTRA, last)):
@@ -510,15 +565,17 @@
     sweeps, blocks, _, span = reflector_vectors.shape
     bw = span // 2
     assert sweeps == 2 and blocks == 2 and rows == span and cols % (2 * WIDTH) == 0
-    assert count % 2 == 0 and bw == 4 * NEAR and ring >= 2
     pairs = cols // (2 * WIDTH)
+    assert count % 2 == 0 and count >= 4 and bw == 4 * NEAR and ring >= 2 and pairs >= 2
     vmem, dma = pltpu.VMEM, pltpu.SemaphoreType.DMA
     return pl.pallas_call(
         functools.partial(kernel, count, ring),
         out_shape=jax.ShapeDtypeStruct((rows, cols), f32),
-        in_specs=[pl.BlockSpec(memory_space=pltpu.SMEM)] + [pl.BlockSpec(memory_space=vmem)] * 3,
+        in_specs=[pl.BlockSpec(memory_space=pltpu.SMEM)] + [pl.BlockSpec(memory_space=pltpu.HBM)] * 3,
         out_specs=pl.BlockSpec(memory_space=vmem),
         scratch_shapes=[
+            vmem((rows, cols), f32), vmem(reflector_vectors.shape, f32),
+            vmem(reflector_factors.shape, f32), dma((3,)),
             vmem((3, bw, bw + 2 * NEAR), f32), vmem((2, bw, bw), f32),
             vmem((2, bw // ring, bw + 2 * NEAR), f32), vmem((bw // ring, bw), f32),
             vmem((2, span, 3 * bw), bf16), vmem((2, span, 3 * bw), bf16),

time: 75.9 us -> 74.2 us (0.978)
  Pallas kernels: 72.5 us -> 70.8 us
    pallas_call x1, Pallas kernels: 72.5 us -> 70.8 us  [per_device(): pl.pallas_call(functools.partial(kernel, count, ring), out_shape=jax.Shap...]
where the time goes in v6:
time: 74.2 us; the launch traced here: 74 us
  Pallas kernels  70.8 us (95%)
  local copies, waits for them, and re-layouts  3.16 us (4%)
    pallas_call x1, Pallas kernels, per_device(): pl.pallas_call(functools.partial(kernel, count, ring), out_shape=jax.Shap...  70.8 us
    unnamed x1, local copies, waits for them, and re-layouts  3.16 us

profile of v6, /device:TPU:0, one launch (start us, length us, event | category | flops | bytes accessed | tf_op | source)
XLA Modules:
  0.0 74.0 jit_solution(15950796258802164858)
XLA Ops:
  0.0 70.8 %shard_map.46 = f32[512,1024]{1,0:T(8,128)} custom-call(s32[2,2]{1,0:T(2,128)} %bounds_ref.1, f32[512,1024]{1,0:T(8,128)} %x_hbm.1, f32[2,2,64,512]{3,2,1,0:T(8,128)} %vec_hbm.1, f32[2,2,64,256]{3,2,1,0:T(8,128)} %fac_hbm.1), custom_call_target="tpu_custom_call" | custom-call | tf_op jit(solution)/shard_map/pallas_call | solution.py:571
  70.8 3.2 %copy.6 = f32[512,1024]{1,0:T(8,128)} copy(f32[512,1024]{1,0:T(8,128)} %shard_map.46) | data formatting | bytes 4194304

commit v7 on v6

--- a/solution.py
+++ b/solution.py
@@ -466,21 +466,28 @@
 
         lax.fori_loop(0, pairs, pair, 0)
 
+    def give(s, q):
+        partner[s, q] = share(s, q)
+        near(s, q).start()
+
     def even_sweep(s):
         def pair(q, carry):
             if s == 0:
                 second_at(even_places, q, 0)
 
-            @pl.when((q < pairs) & inner)
-            def _():
-                if s == 0:
+            if s == 0:
+                @pl.when((q < pairs) & inner)
+                def _():
                     get_initial(q)
-                partner[s, q] = share(s, q)
-                near(s, q).start()
+                    give(0, q)
 
             if s == 0:
                 second_at(even_places, q, 1)
                 build_at(q, jnp.logical_not(ahead))
+
+                @pl.when((q == pairs) & inner & jnp.logical_not(ahead))
+                def _():
+                    lax.fori_loop(0, pairs - 1, lambda r, nothing: (give(1, r), nothing)[1], 0)
 
             @pl.when(q >= 1)
             def _():
@@ -493,6 +500,10 @@
                 @pl.when((q >= 1) & inner)
                 def _():
                     settle(s, q - 1)
+
+                @pl.when((q >= 1) & inner & (ahead | (q == pairs)))
+                def _():
+                    give(1, q - 1)
 
                 @pl.when((q >= 1) & first)
                 def _():

time: 74.2 us -> 72.5 us (0.977)
  Pallas kernels: 70.8 us -> 69.2 us
    pallas_call x1, Pallas kernels: 70.8 us -> 69.2 us  [per_device(): pl.pallas_call(functools.partial(kernel, count, ring), out_shape=jax.Shap...]
where the time goes in v7:
time: 72.5 us; the launch traced here: 72.4 us
  Pallas kernels  69.2 us (95%)
  local copies, waits for them, and re-layouts  3.16 us (4%)
    pallas_call x1, Pallas kernels, per_device(): pl.pallas_call(functools.partial(kernel, count, ring), out_shape=jax.Shap...  69.2 us
    unnamed x1, local copies, waits for them, and re-layouts  3.16 us

profile of v7, /device:TPU:0, one launch (start us, length us, event | category | flops | bytes accessed | tf_op | source)
XLA Modules:
  0.0 72.4 jit_solution(15339432006448442852)
XLA Ops:
  0.0 69.2 %shard_map.46 = f32[512,1024]{1,0:T(8,128)} custom-call(s32[2,2]{1,0:T(2,128)} %bounds_ref.1, f32[512,1024]{1,0:T(8,128)} %x_hbm.1, f32[2,2,64,512]{3,2,1,0:T(8,128)} %vec_hbm.1, f32[2,2,64,256]{3,2,1,0:T(8,128)} %fac_hbm.1), custom_call_target="tpu_custom_call" | custom-call | tf_op jit(solution)/shard_map/pallas_call | solution.py:582
  69.2 3.2 %copy.6 = f32[512,1024]{1,0:T(8,128)} copy(f32[512,1024]{1,0:T(8,128)} %shard_map.46) | data formatting | bytes 4194304
